TPU v7x, 32 devices: a whole 2x2x4 slice. The times are simulated.
32 devices in a mesh: group: 2 (over y), blk: 4 (over z), uly: 4 (over x, core).
Axes of the slice: x: 2, y: 2, z: 4, core: 2. Of those that a mesh axis runs over, the one named last changes fastest.
Arguments:
- query: bfloat16 [768, 3072], P(('group', 'blk', 'uly')), parts along dimension 0, may hold values from -16 to 16
- keys: bfloat16 [768, 3072], P(('group', 'blk', 'uly')), parts along dimension 0, may hold values from -16 to 16
- values: bfloat16 [768, 3072], P(('group', 'blk', 'uly')), parts along dimension 0, may hold values from -6 to 6
- out_weight: bfloat16 [3072, 3072], P('uly', 'blk'), may hold values from -1 to 1
- out_gain: float32 [3072], replicated, may hold values from 0.1 to 1.9
Outputs:
- gated_out: bfloat16 [768, 3072], P(('group', 'blk', 'uly')), parts along dimension 0
There are 2 independent parts, one for each index of `group`. A program takes and returns all parts, laid end to end along the dimension named above; an argument that names none is the same for every part. Nothing has to cross between parts.
All inputs are finite; a program needn't handle non-finite values.
Results may differ from a plain program's by a relative error of at most 0.015.
Values may be sent and summed in bfloat16 or wider, within the bound.
A program may use at most 128 MiB of HBM per device.

v0:
```python
import math

import jax
import jax.numpy as jnp
from jax import lax
from jax.sharding import PartitionSpec as P

HEAD = 64


def make_fold(query_heads, state_now, pieces):
    score_scale = 1.0 / math.sqrt(HEAD)
    head_count = query_heads.shape[1]
    running_max, denominator, weighted = state_now
    key_part, value_part = pieces
    key_count = key_part.shape[0]
    key_heads = key_part.reshape(key_count, head_count, HEAD)
    value_heads = value_part.reshape(key_count, head_count, HEAD)
    scores = (
        jnp.einsum("qhd,khd->qhk", query_heads, key_heads, preferred_element_type=jnp.float32)
        * score_scale
    )
    new_max = jnp.max(scores, axis=2)
    weights = jnp.exp(scores - new_max[:, :, None])
    shrink = jnp.exp(running_max - new_max)
    denominator = denominator * shrink + jnp.sum(weights, axis=2)
    weighted = weighted * shrink[:, :, None] + jnp.einsum(
        "qhk,khd->qhd",
        weights.astype(jnp.bfloat16),
        value_heads,
        preferred_element_type=jnp.float32,
    )
    return (new_max, denominator, weighted)


def initial_state(row_count, head_count):
    return (
        jnp.full((row_count, head_count), -jnp.inf, jnp.float32),
        jnp.zeros((row_count, head_count), jnp.float32),
        jnp.zeros((row_count, head_count, HEAD), jnp.float32),
    )


def on_device(query, keys, values, out_weight, out_gain):
    grouped_q, grouped_k, grouped_v = (
        lax.all_to_all(query, "uly", split_axis=1, concat_axis=0, tiled=True),
        lax.all_to_all(keys, "uly", split_axis=1, concat_axis=0, tiled=True),
        lax.all_to_all(values, "uly", split_axis=1, concat_axis=0, tiled=True),
    )
    row_count = grouped_q.shape[0]
    features = grouped_q.shape[1]
    local_heads = features // HEAD
    query_heads = grouped_q.reshape(row_count, local_heads, HEAD)
    half_heads = local_heads // 2
    half_width = half_heads * HEAD
    low_state = make_fold(
        query_heads[:, :half_heads],
        initial_state(row_count, half_heads),
        (
            lax.all_gather(grouped_k[:, :half_width], "blk", axis=0, tiled=True),
            lax.all_gather(grouped_v[:, :half_width], "blk", axis=0, tiled=True),
        ),
    )
    high_state = make_fold(
        query_heads[:, half_heads:],
        initial_state(row_count, local_heads - half_heads),
        (
            lax.all_gather(grouped_k[:, half_width:], "blk", axis=0, tiled=True),
            lax.all_gather(grouped_v[:, half_width:], "blk", axis=0, tiled=True),
        ),
    )
    denominator = jnp.concatenate([low_state[1], high_state[1]], axis=1)
    weighted = jnp.concatenate([low_state[2], high_state[2]], axis=1)
    attended = (
        (weighted / denominator[:, :, None]).reshape(row_count, features).astype(jnp.bfloat16)
    )
    partial_value = jnp.dot(
        attended,
        lax.all_gather(out_weight, "blk", axis=1, tiled=True),
        preferred_element_type=jnp.float32,
    )
    summed = lax.psum_scatter(
        partial_value.astype(jnp.bfloat16), "uly", scatter_dimension=0, tiled=True
    ).astype(jnp.float32)
    return (out_gain * summed).astype(jnp.bfloat16)


def solution(mesh):
    in_specs = (
        P(("group", "blk", "uly"), None),
        P(("group", "blk", "uly"), None),
        P(("group", "blk", "uly"), None),
        P("uly", "blk"),
        P(),
    )
    out_specs = P(("group", "blk", "uly"), None)
    return jax.shard_map(
        on_device, mesh=mesh, in_specs=in_specs, out_specs=out_specs, check_vma=False
    )
```

profile of v0, /device:TPU:0, one launch (start us, length us, event | category | flops | bytes accessed | tf_op | source)
XLA Modules:
  0.0 152.9 jit_solution(848219083443015823)
XLA Ops:
  6.5 0.0 all-gather.2.cloned.1.call-start
  6.5 0.7 all-gather.2.cloned.1.call-update
  7.3 1.6 %copy.52 = bf16[3,4,8,768]{3,2,0,1:T(8,128)(2,1)} copy(bf16[3,4,8,768]{3,2,1,0:T(8,128)(2,1)} %bitcast.50) | data formatting | bytes 294912 | tf_op jit(solution)/shard_map/all_to_all | solution.py:46
  8.8 4.2 %all-to-all-start.1 = ((bf16[24,4,768]{2,0,1:T(8,128)(2,1)}), bf16[24,4,768]{2,0,1:T(8,128)(2,1)S(1)}, u32[]{:S(2)}, u32[]{:S(2)}) async-start(bf16[24,4,768]{2,0,1:T(8,128)(2,1)} %bitcast.41), calls=%async_computation.1 | async-start | bytes 294912 | tf_op jit(solution)/shard_map/all_to_all | solution.py:46
  13.1 1.6 %copy.51 = bf16[3,4,8,768]{3,2,0,1:T(8,128)(2,1)} copy(bf16[3,4,8,768]{3,2,1,0:T(8,128)(2,1)} %bitcast.51) | data formatting | bytes 294912 | tf_op jit(solution)/shard_map/all_to_all | solution.py:47
  14.6 3.2 %all-to-all-done.1 = bf16[24,4,768]{2,0,1:T(8,128)(2,1)S(1)} async-done(((bf16[24,4,768]{2,0,1:T(8,128)(2,1)}), bf16[24,4,768]{2,0,1:T(8,128)(2,1)S(1)}, u32[]{:S(2)}, u32[]{:S(2)}) %all-to-all-start.1) | async-done | bytes 147488 | tf_op jit(solution)/shard_map/all_to_all | solution.py:46
  17.9 3.3 %all-to-all-start = ((bf16[24,4,768]{2,0,1:T(8,128)(2,1)}), bf16[24,4,768]{2,0,1:T(8,128)(2,1)S(1)}, u32[]{:S(2)}, u32[]{:S(2)}) async-start(bf16[24,4,768]{2,0,1:T(8,128)(2,1)} %bitcast.40), calls=%async_computation | async-start | bytes 294912 | tf_op jit(solution)/shard_map/all_to_all | solution.py:47
  21.2 1.6 %copy.50 = bf16[3,4,8,768]{3,2,0,1:T(8,128)(2,1)} copy(bf16[3,4,8,768]{3,2,1,0:T(8,128)(2,1)} %bitcast.52) | data formatting | bytes 294912 | tf_op jit(solution)/shard_map/all_to_all | solution.py:48
  22.8 0.2 reshape.43
  23.1 2.9 %all-to-all-done = bf16[24,4,768]{2,0,1:T(8,128)(2,1)S(1)} async-done(((bf16[24,4,768]{2,0,1:T(8,128)(2,1)}), bf16[24,4,768]{2,0,1:T(8,128)(2,1)S(1)}, u32[]{:S(2)}, u32[]{:S(2)}) %all-to-all-start) | async-done | bytes 147488 | tf_op jit(solution)/shard_map/all_to_all | solution.py:47
  25.9 3.3 %all-to-all-start.2 = ((bf16[24,4,768]{2,0,1:T(8,128)(2,1)}), bf16[24,4,768]{2,0,1:T(8,128)(2,1)S(1)}, u32[]{:S(2)}, u32[]{:S(2)}) async-start(bf16[24,4,768]{2,0,1:T(8,128)(2,1)} %bitcast.39), calls=%async_computation.2 | async-start | bytes 294912 | tf_op jit(solution)/shard_map/all_to_all | solution.py:48
  29.3 0.0 reduce-scatter.2.cloned.1.call-start
  29.4 21.0 %all_gather.15 = bf16[384,384]{1,0:T(8,128)(2,1)S(1)} all-gather(bf16[96,384]{1,0:T(8,128)(2,1)S(1)} %get-tuple-element.7), channel_id=1, replica_groups=mesh['group'=2,'blk'=4,'uly'=4] {'blk'}, dimensions={0}, use_global_device_ids=true | all-gather | bytes 368640 | tf_op jit(solution)/shard_map/all_gather | solution.py:60
  50.4 0.2 copy.26
  50.6 17.9 %all_gather.17 = bf16[384,384]{1,0:T(8,128)(2,1)S(1)} all-gather(bf16[96,384]{1,0:T(8,128)(2,1)S(1)} %get-tuple-element.8), channel_id=1, replica_groups=mesh['group'=2,'blk'=4,'uly'=4] {'blk'}, dimensions={0}, use_global_device_ids=true | all-gather | bytes 368640 | tf_op jit(solution)/shard_map/all_gather | solution.py:68
  68.5 0.2 copy.31
  68.7 0.0 all-to-all-done.2
  68.8 16.8 %all_gather.16 = bf16[384,384]{1,0:T(8,128)(2,1)S(1)} all-gather(bf16[96,384]{1,0:T(8,128)(2,1)S(1)} %get-tuple-element.9), channel_id=1, replica_groups=mesh['group'=2,'blk'=4,'uly'=4] {'blk'}, dimensions={0}, use_global_device_ids=true | all-gather | bytes 368640 | tf_op jit(solution)/shard_map/all_gather | solution.py:61
  85.6 0.2 copy.30
  85.8 17.5 %all_gather.18 = bf16[384,384]{1,0:T(8,128)(2,1)S(1)} all-gather(bf16[96,384]{1,0:T(8,128)(2,1)S(1)} %get-tuple-element.10), channel_id=1, replica_groups=mesh['group'=2,'blk'=4,'uly'=4] {'blk'}, dimensions={0}, use_global_device_ids=true | all-gather | bytes 368640 | tf_op jit(solution)/shard_map/all_gather | solution.py:69
  103.3 0.2 copy.33
  103.5 0.1 fusion.17
  103.6 0.4 fusion.21
  104.0 0.4 fusion.4
  104.4 0.4 fusion.20
  104.7 0.4 fusion.6
  105.1 0.0 copy-start
  105.1 0.4 fusion.3
  105.5 0.4 fusion.2
  106.0 13.7 %all-gather.2.cloned.1.call-done = bf16[768,3072]{1,0:T(8,128)(2,1)} async-done(((bf16[768,768]{1,0:T(8,128)(2,1)}), bf16[768,3072]{1,0:T(8,128)(2,1)}) %all-gather.2.cloned.1.call-update) | async-done | bytes 4718608 | tf_op jit(solution)/shard_map/all_gather | solution.py:79
  119.7 4.1 %convolution_convert_fusion = bf16[96,3072]{1,0:T(8,128)(2,1)} fusion(bf16[96,768]{0,1:T(8,128)(2,1)S(1)} %bitcast.46, bf16[768,3072]{1,0:T(8,128)(2,1)} %all-gather.2.cloned.1.call-done), kind=kOutput, calls=%fused_computation | convolution fusion | flops 453279744 | bytes 5455872 | tf_op jit(solution)/shard_map/dot_general | solution.py:77
  123.8 0.0 reduce-scatter.2.cloned.1.call-update
  123.8 20.6 %reduce-scatter.2.cloned.1.call-done = bf16[24,3072]{1,0:T(8,128)(2,1)} async-done(((bf16[96,3072]{1,0:T(8,128)(2,1)}), bf16[24,3072]{1,0:T(8,128)(2,1)}) %reduce-scatter.2.cloned.1.call-update) | async-done | bytes 147472 | tf_op jit(solution)/shard_map/reduce_scatter | solution.py:82
  144.4 0.0 copy-done
  144.5 1.6 %multiply_convert_fusion = bf16[24,3072]{1,0:T(8,128)(2,1)} fusion(bf16[24,3072]{1,0:T(8,128)(2,1)} %reduce-scatter.2.cloned.1.call-done, f32[3072]{0:T(1024)S(1)} %copy-done), kind=kLoop, calls=%fused_computation.19 | loop fusion | flops 221184 | bytes 307200 | tf_op jit(solution)/shard_map/convert_element_type | solution.py:85
  (6 shorter events, 0.1 us)
Async XLA Ops:
  6.5 113.2 %all-gather.2.cloned.1.call-start = ((), (), s32[]{:S(2)}) async-start(), calls=%async_computation.4 | async-start | bytes 5898240 | tf_op jit(solution)/shard_map/all_gather | solution.py:79
  8.8 9.0 %all-to-all-start.1 = ((bf16[24,4,768]{2,0,1:T(8,128)(2,1)}), bf16[24,4,768]{2,0,1:T(8,128)(2,1)S(1)}, u32[]{:S(2)}, u32[]{:S(2)}) async-start(bf16[24,4,768]{2,0,1:T(8,128)(2,1)} %bitcast.41), calls=%async_computation.1 | async-start | bytes 294912 | tf_op jit(solution)/shard_map/all_to_all | solution.py:46
  17.9 8.1 %all-to-all-start = ((bf16[24,4,768]{2,0,1:T(8,128)(2,1)}), bf16[24,4,768]{2,0,1:T(8,128)(2,1)S(1)}, u32[]{:S(2)}, u32[]{:S(2)}) async-start(bf16[24,4,768]{2,0,1:T(8,128)(2,1)} %bitcast.40), calls=%async_computation | async-start | bytes 294912 | tf_op jit(solution)/shard_map/all_to_all | solution.py:47
  25.9 42.8 %all-to-all-start.2 = ((bf16[24,4,768]{2,0,1:T(8,128)(2,1)}), bf16[24,4,768]{2,0,1:T(8,128)(2,1)S(1)}, u32[]{:S(2)}, u32[]{:S(2)}) async-start(bf16[24,4,768]{2,0,1:T(8,128)(2,1)} %bitcast.39), calls=%async_computation.2 | async-start | bytes 294912 | tf_op jit(solution)/shard_map/all_to_all | solution.py:48
  29.3 115.2 %reduce-scatter.2.cloned.1.call-start = ((), (), s32[]{:S(2)}) async-start(), calls=%async_computation.5 | async-start | bytes 737280 | tf_op jit(solution)/shard_map/reduce_scatter | solution.py:82
  105.1 39.3 %copy-start = (f32[3072]{0:T(1024)S(1)}, f32[3072]{0:T(1024)}, u32[]{:S(2)}) copy-start(f32[3072]{0:T(1024)} %param.9) | copy-start | bytes 36868
Sparse Core Ops, SparseCore 0:
  8.9 110.7 all-gather.1
  123.9 20.4 reduce-scatter.1
where the time goes:
time: 153 us
  blocking collectives  73.3 us (48%)
  waiting for transfers between devices  41.1 us (27%)
  between operations  13.5 us (9%)
  starting transfers between devices  11 us (7%)
  local copies, waits for them, and re-layouts  6 us (4%)
  matrix products  5.6 us (4%)
  other arithmetic  2.39 us (2%)
    all_gather x1, blocking collectives, on_device(): lax.all_gather(grouped_k[:, :half_width], 'blk', axis=0, tiled=True)  21 us
    reduce_scatter x1, waiting for transfers between devices, on_device(): lax.psum_scatter(partial_value.astype(jnp.bfloat16), 'uly', scatter_dimen...  20.6 us
    all_gather x1, blocking collectives, on_device(): lax.all_gather(grouped_k[:, half_width:], 'blk', axis=0, tiled=True)  17.9 us
    all_gather x1, blocking collectives, on_device(): lax.all_gather(grouped_v[:, half_width:], 'blk', axis=0, tiled=True)  17.5 us
    all_gather x1, blocking collectives, on_device(): lax.all_gather(grouped_v[:, :half_width], 'blk', axis=0, tiled=True)  16.8 us
    all_gather x1, waiting for transfers between devices, on_device(): lax.all_gather(out_weight, 'blk', axis=1, tiled=True)  13.7 us
    all_to_all x1, starting transfers between devices, on_device(): lax.all_to_all(query, 'uly', split_axis=1, concat_axis=0, tiled=True)  4.24 us
    dot_general x1, matrix products, on_device(): jnp.dot(attended, lax.all_gather(out_weight, 'blk', axis=1, tiled=True),...  4.08 us
  transfers between devices with their start and end apart: 5, of which 4 were waited for; matrix products, arithmetic and copies ran while one was open for 5% of the time, Pallas kernels for 0%

commit v1 on v0

--- a/solution.py
+++ b/solution.py
@@ -1,12 +1,16 @@
+import functools
 import math
 
 import jax
 import jax.numpy as jnp
 from jax import lax
+from jax.experimental import pallas as pl
+from jax.experimental.pallas import tpu as pltpu
 from jax.sharding import PartitionSpec as P
 
 HEAD = 64
-
+LANES = 128
+MESH = pl.DeviceIdType.MESH
 
 def make_fold(query_heads, state_now, pieces):
     score_scale = 1.0 / math.sqrt(HEAD)
@@ -85,6 +89,275 @@
     return (out_gain * summed).astype(jnp.bfloat16)
 
 
+def attend_kernel(
+    nb, nu,
+    q_ref, k_ref, v_ref, w_hbm, gain_ref, out_ref,
+    stage_a, stage_b, got_a, got_b, w_ref,
+    att_pair, att_one, att_all, part_f32, part_send, part_got, final_send,
+    w_sem, send_a, send_b, recv_a, recv_b,
+    send_p, recv_p, send_o, recv_o, send_r, recv_r, send_f, recv_f,
+):
+    n = nb * nu
+    rows, width = q_ref.shape
+    tokens = n * rows
+    pairs = stage_a.shape[1] // 3
+    heads = 2 * pairs + 1
+    half = tokens // 2
+    block = nu * rows
+    scale = 1.0 / math.sqrt(HEAD)
+    me_b, me_u = lax.axis_index("blk"), lax.axis_index("uly")
+    me = me_b * nu + me_u
+
+    def there(b, u):
+        return dict(device_id={"blk": b, "uly": u}, device_id_type=MESH)
+
+    barrier = pltpu.get_barrier_semaphore()
+
+    @pl.loop(1, n)
+    def _(d):
+        j = lax.rem(me + d, n)
+        pl.semaphore_signal(barrier, inc=1, **there(j // nu, lax.rem(j, nu)))
+
+    w_copy = pltpu.make_async_copy(w_hbm, w_ref, w_sem)
+    w_copy.start()
+
+    lane = lax.broadcasted_iota(jnp.int32, (rows, LANES), 1)
+    low = lane < HEAD
+    for c in range(n):
+        odd = c % 2
+        first = (heads * c - odd) // 2
+        pair_at = first + odd
+        one_at = first + (0 if odd else pairs)
+        for s, ref in enumerate((q_ref, k_ref, v_ref)):
+            for p in range(pairs):
+                stage_a[c, s * pairs + p] = ref[:, pl.ds((pair_at + p) * LANES, LANES)]
+        q_tile = q_ref[:, pl.ds(one_at * LANES, LANES)]
+        k_tile = k_ref[:, pl.ds(one_at * LANES, LANES)]
+        if odd:
+            stage_b[c, 0] = jnp.concatenate([q_tile[:, HEAD:], k_tile[:, HEAD:]], axis=1)
+        else:
+            stage_b[c, 0] = jnp.concatenate([q_tile[:, :HEAD], k_tile[:, :HEAD]], axis=1)
+        stage_b[c, 1] = v_ref[:, pl.ds(one_at * LANES, LANES)]
+    mine = me_u * nb + me_b
+    got_a[me] = stage_a[mine]
+    got_b[me] = stage_b[mine]
+
+    pl.semaphore_wait(barrier, n - 1)
+
+    def exchange(stage, got, send, recv, d):
+        j = lax.rem(me + d, n)
+        b, u = j // nu, lax.rem(j, nu)
+        return pltpu.make_async_remote_copy(
+            src_ref=stage.at[u * nb + b], dst_ref=got.at[me],
+            send_sem=send.at[d], recv_sem=recv.at[me], **there(b, u))
+
+    def arrival(stage, got, send, recv, d):
+        j = lax.rem(me + n - d, n)
+        return pltpu.make_async_remote_copy(
+            src_ref=stage.at[j], dst_ref=got.at[j],
+            send_sem=send.at[d], recv_sem=recv.at[j], **there(me_b, me_u))
+
+    a_refs = (stage_a, got_a, send_a, recv_a)
+    b_refs = (stage_b, got_b, send_b, recv_b)
+
+    @pl.loop(1, n)
+    def _(d):
+        exchange(*a_refs, d).start()
+
+    @pl.loop(1, n)
+    def _(d):
+        exchange(*b_refs, d).start()
+
+    @pl.loop(1, n)
+    def _(d):
+        arrival(*a_refs, d).wait_recv()
+
+    def softmax(scores):
+        scores = scores * scale
+        top = jnp.max(scores, axis=1, keepdims=True)
+        weights = jnp.exp(scores - top)
+        return weights.astype(jnp.bfloat16), jnp.sum(weights, axis=1, keepdims=True)
+
+    def against(a, b):
+        return lax.dot_general(a, b, (((1,), (1,)), ((), ())), preferred_element_type=jnp.float32)
+
+    wide_low = lax.broadcasted_iota(jnp.int32, (tokens, LANES), 1) < HEAD
+
+    def whole(ref, s):
+        return jnp.concatenate([ref[i, s].astype(jnp.float32) for i in range(n)], axis=0)
+
+    for p in range(pairs):
+        q_all = whole(got_a, p)
+        k_all = whole(got_a, pairs + p).astype(jnp.bfloat16)
+        v_all = whole(got_a, 2 * pairs + p).astype(jnp.bfloat16)
+        pieces = []
+        for keep in (wide_low, jnp.logical_not(wide_low)):
+            q_one = jnp.where(keep, q_all, 0.0).astype(jnp.bfloat16)
+            weights, total = softmax(against(q_one, k_all))
+            pieces.append(jnp.dot(weights, v_all, preferred_element_type=jnp.float32) / total)
+        att_pair[me_b, p] = jnp.where(wide_low, *pieces).astype(jnp.bfloat16)
+
+    def spread(ref, send, recv, d):
+        b = lax.rem(me_b + d, nb)
+        return pltpu.make_async_remote_copy(
+            src_ref=ref.at[me_b], dst_ref=ref.at[me_b],
+            send_sem=send.at[d], recv_sem=recv.at[me_b], **there(b, me_u))
+
+    def spread_in(ref, send, recv, d):
+        b = lax.rem(me_b + nb - d, nb)
+        return pltpu.make_async_remote_copy(
+            src_ref=ref.at[b], dst_ref=ref.at[b],
+            send_sem=send.at[d], recv_sem=recv.at[b], **there(me_b, me_u))
+
+    for d in range(1, nb):
+        spread(att_pair, send_p, recv_p, d).start()
+
+    @pl.loop(1, n)
+    def _(d):
+        arrival(*b_refs, d).wait_recv()
+
+    qk_all = whole(got_b, 0)
+    v_all = whole(got_b, 1).astype(jnp.bfloat16)
+    weights, total = softmax(
+        against(qk_all[:, :HEAD].astype(jnp.bfloat16), qk_all[:, HEAD:].astype(jnp.bfloat16)))
+    wide = jnp.dot(weights, v_all, preferred_element_type=jnp.float32) / total
+    single = jnp.where(lax.rem(me_b, 2) == 0, wide[:, :HEAD], wide[:, HEAD:])
+    att_one[me_b] = jnp.concatenate([single[:half], single[half:]], axis=1).astype(jnp.bfloat16)
+    for d in range(1, nb):
+        spread(att_one, send_o, recv_o, d).start()
+
+    w_copy.wait()
+    for d in range(1, nb):
+        spread_in(att_pair, send_p, recv_p, d).wait_recv()
+    for b in range(nb):
+        odd = b % 2
+        first = (heads * b - odd) // 2 + odd
+        for p in range(pairs):
+            att_all[:, pl.ds((first + p) * LANES, LANES)] = att_pair[b, p]
+    for d in range(1, nb):
+        spread_in(att_one, send_o, recv_o, d).wait_recv()
+    for b in range(0, nb, 2):
+        even, odd = att_one[b], att_one[b + 1]
+        at = pl.ds((heads * b // 2 + pairs) * LANES, LANES)
+        att_all[:half, at] = jnp.concatenate([even[:, :HEAD], odd[:, :HEAD]], axis=1)
+        att_all[half:, at] = jnp.concatenate([even[:, HEAD:], odd[:, HEAD:]], axis=1)
+
+    def scatter(to, d):
+        u = lax.rem(me_u + d, nu)
+        return pltpu.make_async_remote_copy(
+            src_ref=part_send.at[to, u], dst_ref=part_got.at[to, me_u],
+            send_sem=send_r.at[to, d], recv_sem=recv_r.at[to, me_u], **there(me_b, u))
+
+    def scatter_in(to, d):
+        u = lax.rem(me_u + nu - d, nu)
+        return pltpu.make_async_remote_copy(
+            src_ref=part_send.at[to, u], dst_ref=part_got.at[to, u],
+            send_sem=send_r.at[to, d], recv_sem=recv_r.at[to, u], **there(me_b, me_u))
+
+    def final(d):
+        to = lax.rem(me_b + d, nb)
+        return pltpu.make_async_remote_copy(
+            src_ref=final_send.at[to], dst_ref=out_ref.at[me_b],
+            send_sem=send_f.at[d], recv_sem=recv_f.at[me_b], **there(to, me_u))
+
+    def final_in(d):
+        b = lax.rem(me_b + nb - d, nb)
+        return pltpu.make_async_remote_copy(
+            src_ref=final_send.at[b], dst_ref=out_ref.at[b],
+            send_sem=send_f.at[d], recv_sem=recv_f.at[b], **there(me_b, me_u))
+
+    for e in range(1, nb + 1):
+        to = lax.rem(me_b + e, nb)
+        part = jnp.dot(
+            att_all[pl.ds(pl.multiple_of(to * block, block), block), :], w_ref[...],
+            preferred_element_type=jnp.float32)
+        for u in range(nu):
+            one = part[u * rows:(u + 1) * rows]
+            part_f32[to, u] = one
+            part_send[to, u] = one.astype(jnp.bfloat16)
+        for d in range(1, nu):
+            scatter(to, d).start()
+
+    for e in range(1, nb + 1):
+        to = lax.rem(me_b + e, nb)
+        total = part_f32[to, me_u]
+        for d in range(1, nu):
+            scatter_in(to, d).wait_recv()
+            total += part_got[to, lax.rem(me_u + nu - d, nu)].astype(jnp.float32)
+        gated = (gain_ref[me_b] * total).astype(jnp.bfloat16)
+        if e < nb:
+            final_send[to] = gated
+            final(e).start()
+        else:
+            out_ref[me_b] = gated
+
+    for d in range(1, nb):
+        final_in(d).wait_recv()
+
+    @pl.loop(1, n)
+    def _(d):
+        exchange(*a_refs, d).wait_send()
+        exchange(*b_refs, d).wait_send()
+
+    for d in range(1, nb):
+        spread(att_pair, send_p, recv_p, d).wait_send()
+        spread(att_one, send_o, recv_o, d).wait_send()
+        final(d).wait_send()
+    for e in range(1, nb + 1):
+        to = lax.rem(me_b + e, nb)
+        for d in range(1, nu):
+            scatter(to, d).wait_send()
+
+
+def fused(nb, nu, query, keys, values, out_weight, out_gain):
+    n = nb * nu
+    rows, width = query.shape
+    heads = width // HEAD // n
+    pairs = heads // 2
+    depth, columns = out_weight.shape
+    tokens = n * rows
+    bf16, f32 = jnp.bfloat16, jnp.float32
+    vmem, dma = pltpu.VMEM, pltpu.SemaphoreType.DMA
+    in_vmem = pl.BlockSpec(memory_space=pltpu.VMEM)
+    gathered = pl.pallas_call(
+        functools.partial(attend_kernel, nb, nu),
+        out_shape=jax.ShapeDtypeStruct((nb, rows, columns), bf16),
+        in_specs=[in_vmem, in_vmem, in_vmem, pl.BlockSpec(memory_space=pl.ANY), in_vmem],
+        out_specs=in_vmem,
+        scratch_shapes=[
+            vmem((n, 3 * pairs, rows, LANES), bf16),
+            vmem((n, 2, rows, LANES), bf16),
+            vmem((n, 3 * pairs, rows, LANES), bf16),
+            vmem((n, 2, rows, LANES), bf16),
+            vmem((depth, columns), bf16),
+            vmem((nb, pairs, tokens, LANES), bf16),
+            vmem((nb, tokens // 2, LANES), bf16),
+            vmem((tokens, depth), bf16),
+            vmem((nb, nu, rows, columns), f32),
+            vmem((nb, nu, rows, columns), bf16),
+            vmem((nb, nu, rows, columns), bf16),
+            vmem((nb, rows, columns), bf16),
+            dma, dma((n,)), dma((n,)), dma((n,)), dma((n,)),
+            dma((nb,)), dma((nb,)), dma((nb,)), dma((nb,)),
+            dma((nb, nu)), dma((nb, nu)), dma((nb,)), dma((nb,)),
+        ],
+        compiler_params=pltpu.CompilerParams(collective_id=0, has_side_effects=True),
+    )(query, keys, values, out_weight, out_gain.reshape(nb, 1, columns))
+    return gathered.transpose(1, 0, 2).reshape(rows, width)
+
+
+def on_any(nb, nu, query, keys, values, out_weight, out_gain):
+    n = nb * nu
+    rows, width = query.shape
+    heads = width // HEAD
+    suits = (
+        heads % n == 0 and (heads // n) % 2 == 1 and heads // n > 1 and nb % 2 == 0
+        and rows % 8 == 0 and (width // nb) % LANES == 0
+    )
+    plan = functools.partial(fused, nb, nu) if suits else on_device
+    return plan(query, keys, values, out_weight, out_gain)
+
+
 def solution(mesh):
     in_specs = (
         P(("group", "blk", "uly"), None),
@@ -94,6 +367,7 @@
         P(),
     )
     out_specs = P(("group", "blk", "uly"), None)
+    body = functools.partial(on_any, mesh.shape["blk"], mesh.shape["uly"])
     return jax.shard_map(
-        on_device, mesh=mesh, in_specs=in_specs, out_specs=out_specs, check_vma=False
-    )
+        body, mesh=mesh, in_specs=in_specs, out_specs=out_specs, check_vma=False
+    )

time: 153 us -> 45.3 us (0.30)
  blocking collectives: 73.3 us -> 0 us
  Pallas kernels: 0 us -> 43.6 us
  waiting for transfers between devices: 41.1 us -> 0 us
  between operations: 13.5 us -> 0.01 us
  starting transfers between devices: 11 us -> 0 us
  matrix products: 5.6 us -> 0 us
  local copies, waits for them, and re-layouts: 6 us -> 1.58 us
  other arithmetic: 2.39 us -> 0 us
    all_gather x4 -> x0, blocking collectives: 73.3 us -> none  [the longest x1 21 us: on_device(): lax.all_gather(grouped_k[:, :half_width], 'blk', axis=0, tiled=True)]
    pallas_call x0 -> x1, Pallas kernels: none -> 43.6 us  [fused(): pl.pallas_call(functools.partial(attend_kernel, nb, nu), out_shape=jax.Sh...]
    reduce_scatter x1 -> x0, waiting for transfers between devices: 20.6 us -> none  [on_device(): lax.psum_scatter(partial_value.astype(jnp.bfloat16), 'uly', scatter_dimen...]
    all_gather x1 -> x0, waiting for transfers between devices: 13.7 us -> none  [on_device(): lax.all_gather(out_weight, 'blk', axis=1, tiled=True)]
    all_to_all x3 -> x0, starting transfers between devices: 10.9 us -> none  [the longest x1 4.24 us: on_device(): lax.all_to_all(query, 'uly', split_axis=1, concat_axis=0, tiled=True)]
    all_to_all x3 -> x0, waiting for transfers between devices: 6.09 us -> none  [the longest x1 3.2 us: on_device(): lax.all_to_all(query, 'uly', split_axis=1, concat_axis=0, tiled=True)]
    dot_general x5 -> x0, matrix products: 5.6 us -> none  [the longest x1 4.08 us: on_device(): jnp.dot(attended, lax.all_gather(out_weight, 'blk', axis=1, tiled=True),...]
    all_to_all x3 -> x0, local copies, waits for them, and re-layouts: 4.76 us -> none  [the longest x1 1.6 us: on_device(): lax.all_to_all(values, 'uly', split_axis=1, concat_axis=0, tiled=True)]
  transfers between devices with their start and end apart: 5 -> 0, of which waited for: 4 -> 0; matrix products, arithmetic and copies ran while one was open for 5% -> 0% of each run, Pallas kernels for 0% -> 0%
where the time goes in v1:
time: 45.3 us; the launch traced here: 45.2 us
  Pallas kernels  43.6 us (96%)
  local copies, waits for them, and re-layouts  1.58 us (3%)
    pallas_call x1, Pallas kernels, fused(): pl.pallas_call(functools.partial(attend_kernel, nb, nu), out_shape=jax.Sh...  43.6 us
    reshape x1, local copies, waits for them, and re-layouts, fused(): return gathered.transpose(1, 0, 2).reshape(rows, width)  1.58 us

profile of v1, /device:TPU:0, one launch (start us, length us, event | category | flops | bytes accessed | tf_op | source)
XLA Modules:
  0.0 45.2 jit_solution(17797296293280347043)
XLA Ops:
  0.0 43.6 %shard_map.55 = bf16[4,24,768]{2,1,0:T(8,128)(2,1)} custom-call(bf16[24,3072]{1,0:T(8,128)(2,1)} %q_ref.1, bf16[24,3072]{1,0:T(8,128)(2,1)} %k_ref.1, bf16[24,3072]{1,0:T(8,128)(2,1)} %v_ref.1, bf16[768,768]{1,0:T(8,128)(2,1)} %w_hbm.1, f32[4,1,768]{2,1,0:T(1,128)} %bitcast.5), custom_call_target="tpu_custom_call" | custom-call | tf_op jit(solution)/shard_map/pallas_call | solution.py:322
  43.6 1.6 %copy.7 = bf16[4,3,8,768]{3,2,0,1:T(8,128)(2,1)} copy(bf16[4,3,8,768]{3,2,1,0:T(8,128)(2,1)} %bitcast.4) | data formatting | bytes 294912 | tf_op jit(solution)/shard_map/reshape | solution.py:346

commit v2 on v1

--- a/solution.py
+++ b/solution.py
@@ -91,22 +91,29 @@
 
 def attend_kernel(
     nb, nu,
-    q_ref, k_ref, v_ref, w_hbm, gain_ref, out_ref,
-    stage_a, stage_b, got_a, got_b, w_ref,
+    q_hbm, k_hbm, v_hbm, w_hbm, gain_ref, out_ref,
+    q_ref, k_ref, v_ref, stage_a, stage_b, got_a, got_b, w_ref,
     att_pair, att_one, att_all, part_f32, part_send, part_got, final_send,
-    w_sem, send_a, send_b, recv_a, recv_b,
-    send_p, recv_p, send_o, recv_o, send_r, recv_r, send_f, recv_f,
+    in_sem, send_a, send_b, recv_a, recv_b,
+    send_p, recv_p, send_o, recv_o, pass_p, pass_o, send_r, recv_r, send_f, recv_f,
 ):
     n = nb * nu
     rows, width = q_ref.shape
     tokens = n * rows
     pairs = stage_a.shape[1] // 3
     heads = 2 * pairs + 1
-    half = tokens // 2
     block = nu * rows
+    half = block // 2
+    side = nb // 2
+    upper = (rows // 8 + 1) // 2 * 8
+    order = sorted(range(nb), key=lambda t: -abs(2 * t - nb + 1))
     scale = 1.0 / math.sqrt(HEAD)
     me_b, me_u = lax.axis_index("blk"), lax.axis_index("uly")
     me = me_b * nu + me_u
+    my_side = me_b // side
+    gate_here = (side - 1) + my_side
+    gate_there = side - my_side
+    is_gate = me_b == gate_here
 
     def there(b, u):
         return dict(device_id={"blk": b, "uly": u}, device_id_type=MESH)
@@ -118,11 +125,16 @@
         j = lax.rem(me + d, n)
         pl.semaphore_signal(barrier, inc=1, **there(j // nu, lax.rem(j, nu)))
 
-    w_copy = pltpu.make_async_copy(w_hbm, w_ref, w_sem)
-    w_copy.start()
-
-    lane = lax.broadcasted_iota(jnp.int32, (rows, LANES), 1)
-    low = lane < HEAD
+    loads = [
+        pltpu.make_async_copy(src, dst, in_sem.at[i])
+        for i, (src, dst) in enumerate(
+            ((q_hbm, q_ref), (k_hbm, k_ref), (v_hbm, v_ref), (w_hbm, w_ref)))
+    ]
+    for load in loads:
+        load.start()
+    for load in loads[:3]:
+        load.wait()
+
     for c in range(n):
         odd = c % 2
         first = (heads * c - odd) // 2
@@ -131,13 +143,15 @@
         for s, ref in enumerate((q_ref, k_ref, v_ref)):
             for p in range(pairs):
                 stage_a[c, s * pairs + p] = ref[:, pl.ds((pair_at + p) * LANES, LANES)]
-        q_tile = q_ref[:, pl.ds(one_at * LANES, LANES)]
-        k_tile = k_ref[:, pl.ds(one_at * LANES, LANES)]
-        if odd:
-            stage_b[c, 0] = jnp.concatenate([q_tile[:, HEAD:], k_tile[:, HEAD:]], axis=1)
-        else:
-            stage_b[c, 0] = jnp.concatenate([q_tile[:, :HEAD], k_tile[:, :HEAD]], axis=1)
-        stage_b[c, 1] = v_ref[:, pl.ds(one_at * LANES, LANES)]
+        q_one, k_one, v_one = (
+            ref[:, pl.ds(one_at * LANES, LANES)].astype(jnp.float32)[:, odd * HEAD:(odd + 1) * HEAD]
+            for ref in (q_ref, k_ref, v_ref))
+        rest = jnp.concatenate(
+            [v_one[upper:], jnp.zeros((2 * upper - rows, HEAD), jnp.float32)]
+            if 2 * upper > rows else [v_one[upper:]], axis=0)
+        stage_b[c] = jnp.concatenate(
+            [jnp.concatenate([q_one, k_one], axis=1), jnp.concatenate([v_one[:upper], rest], axis=1)],
+            axis=0).astype(jnp.bfloat16)
     mine = me_u * nb + me_b
     got_a[me] = stage_a[mine]
     got_b[me] = stage_b[mine]
@@ -195,52 +209,56 @@
             q_one = jnp.where(keep, q_all, 0.0).astype(jnp.bfloat16)
             weights, total = softmax(against(q_one, k_all))
             pieces.append(jnp.dot(weights, v_all, preferred_element_type=jnp.float32) / total)
-        att_pair[me_b, p] = jnp.where(wide_low, *pieces).astype(jnp.bfloat16)
-
-    def spread(ref, send, recv, d):
-        b = lax.rem(me_b + d, nb)
-        return pltpu.make_async_remote_copy(
-            src_ref=ref.at[me_b], dst_ref=ref.at[me_b],
-            send_sem=send.at[d], recv_sem=recv.at[me_b], **there(b, me_u))
-
-    def spread_in(ref, send, recv, d):
-        b = lax.rem(me_b + nb - d, nb)
-        return pltpu.make_async_remote_copy(
-            src_ref=ref.at[b], dst_ref=ref.at[b],
-            send_sem=send.at[d], recv_sem=recv.at[b], **there(me_b, me_u))
-
-    for d in range(1, nb):
-        spread(att_pair, send_p, recv_p, d).start()
+        joined = jnp.where(wide_low, *pieces).astype(jnp.bfloat16)
+        for t in range(nb):
+            att_pair[me_b, t, p] = joined[t * block:(t + 1) * block]
+
+    def target(d):
+        return gate_there if d == 0 else my_side * side + lax.rem(me_b + d, side)
+
+    def spread(ref, send, recv, d, t):
+        return pltpu.make_async_remote_copy(
+            src_ref=ref.at[me_b, t], dst_ref=ref.at[me_b, t],
+            send_sem=send.at[d, t], recv_sem=recv.at[me_b, t], **there(target(d), me_u))
+
+    def spread_in(ref, send, recv, b, t):
+        return pltpu.make_async_remote_copy(
+            src_ref=ref.at[b, t], dst_ref=ref.at[b, t],
+            send_sem=send.at[0, t], recv_sem=recv.at[b, t], **there(me_b, me_u))
+
+    def pass_on(ref, sems, recv, d, far, t):
+        return pltpu.make_async_remote_copy(
+            src_ref=ref.at[far, t], dst_ref=ref.at[far, t],
+            send_sem=sems.at[d, far, t], recv_sem=recv.at[far, t], **there(target(d), me_u))
+
+    pair_refs, one_refs = (att_pair, send_p, recv_p), (att_one, send_o, recv_o)
+    early = order[:side]
+    for t in early:
+        for d in range(side):
+            spread(*pair_refs, d, t).start()
 
     @pl.loop(1, n)
     def _(d):
         arrival(*b_refs, d).wait_recv()
 
-    qk_all = whole(got_b, 0)
-    v_all = whole(got_b, 1).astype(jnp.bfloat16)
+    got = [got_b[i].astype(jnp.float32) for i in range(n)]
+    qk_all = jnp.concatenate([g[:rows] for g in got], axis=0)
+    v_all = jnp.concatenate(
+        [piece for g in got
+         for piece in (g[rows:, :HEAD], g[rows:2 * rows - upper, HEAD:])], axis=0)
     weights, total = softmax(
         against(qk_all[:, :HEAD].astype(jnp.bfloat16), qk_all[:, HEAD:].astype(jnp.bfloat16)))
-    wide = jnp.dot(weights, v_all, preferred_element_type=jnp.float32) / total
-    single = jnp.where(lax.rem(me_b, 2) == 0, wide[:, :HEAD], wide[:, HEAD:])
-    att_one[me_b] = jnp.concatenate([single[:half], single[half:]], axis=1).astype(jnp.bfloat16)
-    for d in range(1, nb):
-        spread(att_one, send_o, recv_o, d).start()
-
-    w_copy.wait()
-    for d in range(1, nb):
-        spread_in(att_pair, send_p, recv_p, d).wait_recv()
-    for b in range(nb):
-        odd = b % 2
-        first = (heads * b - odd) // 2 + odd
-        for p in range(pairs):
-            att_all[:, pl.ds((first + p) * LANES, LANES)] = att_pair[b, p]
-    for d in range(1, nb):
-        spread_in(att_one, send_o, recv_o, d).wait_recv()
-    for b in range(0, nb, 2):
-        even, odd = att_one[b], att_one[b + 1]
-        at = pl.ds((heads * b // 2 + pairs) * LANES, LANES)
-        att_all[:half, at] = jnp.concatenate([even[:, :HEAD], odd[:, :HEAD]], axis=1)
-        att_all[half:, at] = jnp.concatenate([even[:, HEAD:], odd[:, HEAD:]], axis=1)
+    single = jnp.dot(
+        weights, v_all.astype(jnp.bfloat16), preferred_element_type=jnp.float32) / total
+    for t in range(nb):
+        at = t * block
+        att_one[me_b, t] = jnp.concatenate(
+            [single[at:at + half], single[at + half:at + block]], axis=1).astype(jnp.bfloat16)
+    for t in order:
+        for d in range(side):
+            if t not in early:
+                spread(*pair_refs, d, t).start()
+            spread(*one_refs, d, t).start()
 
     def scatter(to, d):
         u = lax.rem(me_u + d, nu)
@@ -254,42 +272,71 @@
             src_ref=part_send.at[to, u], dst_ref=part_got.at[to, u],
             send_sem=send_r.at[to, d], recv_sem=recv_r.at[to, u], **there(me_b, me_u))
 
-    def final(d):
-        to = lax.rem(me_b + d, nb)
+    def final(to):
         return pltpu.make_async_remote_copy(
             src_ref=final_send.at[to], dst_ref=out_ref.at[me_b],
-            send_sem=send_f.at[d], recv_sem=recv_f.at[me_b], **there(to, me_u))
+            send_sem=send_f.at[to], recv_sem=recv_f.at[me_b], **there(to, me_u))
 
     def final_in(d):
         b = lax.rem(me_b + nb - d, nb)
         return pltpu.make_async_remote_copy(
             src_ref=final_send.at[b], dst_ref=out_ref.at[b],
-            send_sem=send_f.at[d], recv_sem=recv_f.at[b], **there(me_b, me_u))
-
-    for e in range(1, nb + 1):
-        to = lax.rem(me_b + e, nb)
-        part = jnp.dot(
-            att_all[pl.ds(pl.multiple_of(to * block, block), block), :], w_ref[...],
-            preferred_element_type=jnp.float32)
-        for u in range(nu):
-            one = part[u * rows:(u + 1) * rows]
-            part_f32[to, u] = one
-            part_send[to, u] = one.astype(jnp.bfloat16)
-        for d in range(1, nu):
-            scatter(to, d).start()
-
-    for e in range(1, nb + 1):
-        to = lax.rem(me_b + e, nb)
+            send_sem=send_f.at[b], recv_sem=recv_f.at[b], **there(me_b, me_u))
+
+    def reduce(to):
         total = part_f32[to, me_u]
         for d in range(1, nu):
             scatter_in(to, d).wait_recv()
             total += part_got[to, lax.rem(me_u + nu - d, nu)].astype(jnp.float32)
         gated = (gain_ref[me_b] * total).astype(jnp.bfloat16)
-        if e < nb:
+
+        @pl.when(me_b == to)
+        def _():
+            out_ref[to] = gated
+
+        @pl.when(me_b != to)
+        def _():
             final_send[to] = gated
-            final(e).start()
-        else:
-            out_ref[me_b] = gated
+            final(to).start()
+
+    loads[3].wait()
+    far_side = (1 - my_side) * side
+    for turn, t in enumerate(order):
+        for refs, sems in ((pair_refs, pass_p), (one_refs, pass_o)):
+            for i in range(side):
+                far = far_side + i
+                spread_in(*refs, far, t).wait_recv()
+
+                @pl.when(is_gate)
+                def _():
+                    for d in range(1, side):
+                        pass_on(refs[0], sems, refs[2], d, far, t).start()
+        for d in range(1, side):
+            near = target(d)
+            spread_in(*pair_refs, near, t).wait_recv()
+            spread_in(*one_refs, near, t).wait_recv()
+        for b in range(0, nb, 2):
+            tile = heads * b // 2
+            for p in range(pairs):
+                att_all[:, pl.ds((tile + p) * LANES, LANES)] = att_pair[b, t, p]
+                att_all[:, pl.ds((tile + pairs + 1 + p) * LANES, LANES)] = att_pair[b + 1, t, p]
+            even, odd = att_one[b, t].astype(jnp.float32), att_one[b + 1, t].astype(jnp.float32)
+            at = pl.ds((tile + pairs) * LANES, LANES)
+            att_all[:, at] = jnp.concatenate(
+                [jnp.concatenate([even[:, :HEAD], odd[:, :HEAD]], axis=1),
+                 jnp.concatenate([even[:, HEAD:], odd[:, HEAD:]], axis=1)],
+                axis=0).astype(jnp.bfloat16)
+        part = jnp.dot(att_all[...], w_ref[...], preferred_element_type=jnp.float32)
+        for u in range(nu):
+            one = part[u * rows:(u + 1) * rows]
+            part_f32[t, u] = one
+            part_send[t, u] = one.astype(jnp.bfloat16)
+        for d in range(1, nu):
+            scatter(t, d).start()
+        if turn >= 2:
+            reduce(order[turn - 2])
+    for t in order[-2:]:
+        reduce(t)
 
     for d in range(1, nb):
         final_in(d).wait_recv()
@@ -299,14 +346,23 @@
         exchange(*a_refs, d).wait_send()
         exchange(*b_refs, d).wait_send()
 
-    for d in range(1, nb):
-        spread(att_pair, send_p, recv_p, d).wait_send()
-        spread(att_one, send_o, recv_o, d).wait_send()
-        final(d).wait_send()
-    for e in range(1, nb + 1):
-        to = lax.rem(me_b + e, nb)
+    for t in range(nb):
+        for d in range(side):
+            spread(*pair_refs, d, t).wait_send()
+            spread(*one_refs, d, t).wait_send()
         for d in range(1, nu):
-            scatter(to, d).wait_send()
+            scatter(t, d).wait_send()
+
+        @pl.when(me_b != t)
+        def _():
+            final(t).wait_send()
+
+        @pl.when(is_gate)
+        def _():
+            for i in range(side):
+                for d in range(1, side):
+                    pass_on(att_pair, pass_p, recv_p, d, far_side + i, t).wait_send()
+                    pass_on(att_one, pass_o, recv_o, d, far_side + i, t).wait_send()
 
 
 def fused(nb, nu, query, keys, values, out_weight, out_gain):
@@ -315,30 +371,34 @@
     heads = width // HEAD // n
     pairs = heads // 2
     depth, columns = out_weight.shape
-    tokens = n * rows
     bf16, f32 = jnp.bfloat16, jnp.float32
     vmem, dma = pltpu.VMEM, pltpu.SemaphoreType.DMA
     in_vmem = pl.BlockSpec(memory_space=pltpu.VMEM)
+    in_place = pl.BlockSpec(memory_space=pl.ANY)
+    block, side = nu * rows, nb // 2
+    upper = (rows // 8 + 1) // 2 * 8
     gathered = pl.pallas_call(
         functools.partial(attend_kernel, nb, nu),
         out_shape=jax.ShapeDtypeStruct((nb, rows, columns), bf16),
-        in_specs=[in_vmem, in_vmem, in_vmem, pl.BlockSpec(memory_space=pl.ANY), in_vmem],
+        in_specs=[in_place, in_place, in_place, in_place, in_vmem],
         out_specs=in_vmem,
         scratch_shapes=[
+            vmem((rows, width), bf16), vmem((rows, width), bf16), vmem((rows, width), bf16),
             vmem((n, 3 * pairs, rows, LANES), bf16),
-            vmem((n, 2, rows, LANES), bf16),
+            vmem((n, rows + upper, LANES), bf16),
             vmem((n, 3 * pairs, rows, LANES), bf16),
-            vmem((n, 2, rows, LANES), bf16),
+            vmem((n, rows + upper, LANES), bf16),
             vmem((depth, columns), bf16),
-            vmem((nb, pairs, tokens, LANES), bf16),
-            vmem((nb, tokens // 2, LANES), bf16),
-            vmem((tokens, depth), bf16),
+            vmem((nb, nb, pairs, block, LANES), bf16),
+            vmem((nb, nb, block // 2, LANES), bf16),
+            vmem((block, depth), bf16),
             vmem((nb, nu, rows, columns), f32),
             vmem((nb, nu, rows, columns), bf16),
             vmem((nb, nu, rows, columns), bf16),
             vmem((nb, rows, columns), bf16),
-            dma, dma((n,)), dma((n,)), dma((n,)), dma((n,)),
-            dma((nb,)), dma((nb,)), dma((nb,)), dma((nb,)),
+            dma((4,)), dma((n,)), dma((n,)), dma((n,)), dma((n,)),
+            dma((side, nb)), dma((nb, nb)), dma((side, nb)), dma((nb, nb)),
+            dma((side, nb, nb)), dma((side, nb, nb)),
             dma((nb, nu)), dma((nb, nu)), dma((nb,)), dma((nb,)),
         ],
         compiler_params=pltpu.CompilerParams(collective_id=0, has_side_effects=True),

time: 45.3 us -> 43.2 us (0.954)
  Pallas kernels: 43.6 us -> 41.4 us
    pallas_call x1, Pallas kernels: 43.6 us -> 41.4 us  [fused(): pl.pallas_call(functools.partial(attend_kernel, nb, nu), out_shape=jax.Sh...]
where the time goes in v2:
time: 43.2 us; the launch traced here: 43 us
  Pallas kernels  41.4 us (96%)
  local copies, waits for them, and re-layouts  1.58 us (4%)
    pallas_call x1, Pallas kernels, fused(): pl.pallas_call(functools.partial(attend_kernel, nb, nu), out_shape=jax.Sh...  41.4 us
    reshape x1, local copies, waits for them, and re-layouts, fused(): return gathered.transpose(1, 0, 2).reshape(rows, width)  1.58 us

profile of v2, /device:TPU:0, one launch (start us, length us, event | category | flops | bytes accessed | tf_op | source)
XLA Modules:
  0.0 43.0 jit_solution(13518584542691314191)
XLA Ops:
  0.0 41.4 %shard_map.55 = bf16[4,24,768]{2,1,0:T(8,128)(2,1)} custom-call(bf16[24,3072]{1,0:T(8,128)(2,1)} %q_hbm.1, bf16[24,3072]{1,0:T(8,128)(2,1)} %k_hbm.1, bf16[24,3072]{1,0:T(8,128)(2,1)} %v_hbm.1, bf16[768,768]{1,0:T(8,128)(2,1)} %w_hbm.1, f32[4,1,768]{2,1,0:T(1,128)} %bitcast.5), custom_call_target="tpu_custom_call" | custom-call | tf_op jit(solution)/shard_map/pallas_call | solution.py:380
  41.4 1.6 %copy.7 = bf16[4,3,8,768]{3,2,0,1:T(8,128)(2,1)} copy(bf16[4,3,8,768]{3,2,1,0:T(8,128)(2,1)} %bitcast.4) | data formatting | bytes 294912 | tf_op jit(solution)/shard_map/reshape | solution.py:406

commit v3 on v2

--- a/solution.py
+++ b/solution.py
@@ -106,7 +106,6 @@
     half = block // 2
     side = nb // 2
     upper = (rows // 8 + 1) // 2 * 8
-    order = sorted(range(nb), key=lambda t: -abs(2 * t - nb + 1))
     scale = 1.0 / math.sqrt(HEAD)
     me_b, me_u = lax.axis_index("blk"), lax.axis_index("uly")
     me = me_b * nu + me_u
@@ -114,6 +113,10 @@
     gate_here = (side - 1) + my_side
     gate_there = side - my_side
     is_gate = me_b == gate_here
+
+    def turn_of(b, e):
+        upward = b // side
+        return upward * e + (1 - upward) * (nb - 1 - e)
 
     def there(b, u):
         return dict(device_id={"blk": b, "uly": u}, device_id_type=MESH)
@@ -158,29 +161,24 @@
 
     pl.semaphore_wait(barrier, n - 1)
 
-    def exchange(stage, got, send, recv, d):
-        j = lax.rem(me + d, n)
-        b, u = j // nu, lax.rem(j, nu)
+    def exchange(stage, got, send, recv, b, u):
         return pltpu.make_async_remote_copy(
             src_ref=stage.at[u * nb + b], dst_ref=got.at[me],
-            send_sem=send.at[d], recv_sem=recv.at[me], **there(b, u))
+            send_sem=send.at[b * nu + u], recv_sem=recv.at[me], **there(b, u))
 
     def arrival(stage, got, send, recv, d):
         j = lax.rem(me + n - d, n)
         return pltpu.make_async_remote_copy(
             src_ref=stage.at[j], dst_ref=got.at[j],
-            send_sem=send.at[d], recv_sem=recv.at[j], **there(me_b, me_u))
+            send_sem=send.at[j], recv_sem=recv.at[j], **there(me_b, me_u))
 
     a_refs = (stage_a, got_a, send_a, recv_a)
     b_refs = (stage_b, got_b, send_b, recv_b)
 
-    @pl.loop(1, n)
-    def _(d):
-        exchange(*a_refs, d).start()
-
-    @pl.loop(1, n)
-    def _(d):
-        exchange(*b_refs, d).start()
+    for refs in (a_refs, b_refs):
+        for d in range(1, n):
+            j = lax.rem(me_b + d // nu, nb) * nu + lax.rem(me_u + d % nu, nu)
+            exchange(*refs, j // nu, lax.rem(j, nu)).start()
 
     @pl.loop(1, n)
     def _(d):
@@ -216,7 +214,8 @@
     def target(d):
         return gate_there if d == 0 else my_side * side + lax.rem(me_b + d, side)
 
-    def spread(ref, send, recv, d, t):
+    def spread(ref, send, recv, d, e):
+        t = turn_of(target(d), e)
         return pltpu.make_async_remote_copy(
             src_ref=ref.at[me_b, t], dst_ref=ref.at[me_b, t],
             send_sem=send.at[d, t], recv_sem=recv.at[me_b, t], **there(target(d), me_u))
@@ -232,10 +231,12 @@
             send_sem=sems.at[d, far, t], recv_sem=recv.at[far, t], **there(target(d), me_u))
 
     pair_refs, one_refs = (att_pair, send_p, recv_p), (att_one, send_o, recv_o)
-    early = order[:side]
-    for t in early:
+    plan = [(0, e) for e in range(side)] + [(1, e) for e in range(side)]
+    plan += [(kind, e) for e in range(side, nb) for kind in (0, 1)]
+    both = ((*pair_refs, pass_p), (*one_refs, pass_o))
+    for kind, e in plan[:side]:
         for d in range(side):
-            spread(*pair_refs, d, t).start()
+            spread(*both[kind][:3], d, e).start()
 
     @pl.loop(1, n)
     def _(d):
@@ -254,11 +255,9 @@
         at = t * block
         att_one[me_b, t] = jnp.concatenate(
             [single[at:at + half], single[at + half:at + block]], axis=1).astype(jnp.bfloat16)
-    for t in order:
+    for kind, e in plan[side:]:
         for d in range(side):
-            if t not in early:
-                spread(*pair_refs, d, t).start()
-            spread(*one_refs, d, t).start()
+            spread(*both[kind][:3], d, e).start()
 
     def scatter(to, d):
         u = lax.rem(me_u + d, nu)
@@ -283,7 +282,8 @@
             src_ref=final_send.at[b], dst_ref=out_ref.at[b],
             send_sem=send_f.at[b], recv_sem=recv_f.at[b], **there(me_b, me_u))
 
-    def reduce(to):
+    def reduce(e):
+        to = turn_of(me_b, e)
         total = part_f32[to, me_u]
         for d in range(1, nu):
             scatter_in(to, d).wait_recv()
@@ -301,16 +301,19 @@
 
     loads[3].wait()
     far_side = (1 - my_side) * side
-    for turn, t in enumerate(order):
-        for refs, sems in ((pair_refs, pass_p), (one_refs, pass_o)):
-            for i in range(side):
-                far = far_side + i
-                spread_in(*refs, far, t).wait_recv()
-
-                @pl.when(is_gate)
-                def _():
-                    for d in range(1, side):
-                        pass_on(refs[0], sems, refs[2], d, far, t).start()
+    for kind, turn in plan:
+        t = turn_of(me_b, turn)
+        ref, send, recv, passed = both[kind]
+        for i in range(side):
+            far = far_side + i
+            spread_in(ref, send, recv, far, t).wait_recv()
+
+            @pl.when(is_gate)
+            def _():
+                for d in range(1, side):
+                    pass_on(ref, passed, recv, d, far, t).start()
+        if kind == 0:
+            continue
         for d in range(1, side):
             near = target(d)
             spread_in(*pair_refs, near, t).wait_recv()
@@ -334,17 +337,18 @@
         for d in range(1, nu):
             scatter(t, d).start()
         if turn >= 2:
-            reduce(order[turn - 2])
-    for t in order[-2:]:
-        reduce(t)
+            reduce(turn - 2)
+    for turn in range(nb - 2, nb):
+        reduce(turn)
 
     for d in range(1, nb):
         final_in(d).wait_recv()
 
     @pl.loop(1, n)
     def _(d):
-        exchange(*a_refs, d).wait_send()
-        exchange(*b_refs, d).wait_send()
+        j = lax.rem(me + d, n)
+        exchange(*a_refs, j // nu, lax.rem(j, nu)).wait_send()
+        exchange(*b_refs, j // nu, lax.rem(j, nu)).wait_send()
 
     for t in range(nb):
         for d in range(side):

time: 43.2 us -> 39.8 us (0.921)
  Pallas kernels: 41.4 us -> 38 us
    pallas_call x1, Pallas kernels: 41.4 us -> 38 us  [fused(): pl.pallas_call(functools.partial(attend_kernel, nb, nu), out_shape=jax.Sh...]
where the time goes in v3:
time: 39.8 us; the launch traced here: 39.6 us
  Pallas kernels  38 us (95%)
  local copies, waits for them, and re-layouts  1.58 us (4%)
    pallas_call x1, Pallas kernels, fused(): pl.pallas_call(functools.partial(attend_kernel, nb, nu), out_shape=jax.Sh...  38 us
    reshape x1, local copies, waits for them, and re-layouts, fused(): return gathered.transpose(1, 0, 2).reshape(rows, width)  1.58 us

profile of v3, /device:TPU:0, one launch (start us, length us, event | category | flops | bytes accessed | tf_op | source)
XLA Modules:
  0.0 39.6 jit_solution(10833981016856922608)
XLA Ops:
  0.0 38.0 %shard_map.55 = bf16[4,24,768]{2,1,0:T(8,128)(2,1)} custom-call(bf16[24,3072]{1,0:T(8,128)(2,1)} %q_hbm.1, bf16[24,3072]{1,0:T(8,128)(2,1)} %k_hbm.1, bf16[24,3072]{1,0:T(8,128)(2,1)} %v_hbm.1, bf16[768,768]{1,0:T(8,128)(2,1)} %w_hbm.1, f32[4,1,768]{2,1,0:T(1,128)} %bitcast.5), custom_call_target="tpu_custom_call" | custom-call | tf_op jit(solution)/shard_map/pallas_call | solution.py:384
  38.0 1.6 %copy.7 = bf16[4,3,8,768]{3,2,0,1:T(8,128)(2,1)} copy(bf16[4,3,8,768]{3,2,1,0:T(8,128)(2,1)} %bitcast.4) | data formatting | bytes 294912 | tf_op jit(solution)/shard_map/reshape | solution.py:410

commit v4 on v3

--- a/solution.py
+++ b/solution.py
@@ -176,9 +176,8 @@
     b_refs = (stage_b, got_b, send_b, recv_b)
 
     for refs in (a_refs, b_refs):
-        for d in range(1, n):
-            j = lax.rem(me_b + d // nu, nb) * nu + lax.rem(me_u + d % nu, nu)
-            exchange(*refs, j // nu, lax.rem(j, nu)).start()
+        for d in range(n - 1, 0, -1):
+            exchange(*refs, lax.rem(me_b + d // nu, nb), lax.rem(me_u + d % nu, nu)).start()
 
     @pl.loop(1, n)
     def _(d):

time: 39.8 us -> 39.3 us (0.987)
  Pallas kernels: 38 us -> 37.5 us
    pallas_call x1, Pallas kernels: 38 us -> 37.5 us  [fused(): pl.pallas_call(functools.partial(attend_kernel, nb, nu), out_shape=jax.Sh...]
where the time goes in v4:
time: 39.3 us; the launch traced here: 39.1 us
  Pallas kernels  37.5 us (95%)
  local copies, waits for them, and re-layouts  1.58 us (4%)
    pallas_call x1, Pallas kernels, fused(): pl.pallas_call(functools.partial(attend_kernel, nb, nu), out_shape=jax.Sh...  37.5 us
    reshape x1, local copies, waits for them, and re-layouts, fused(): return gathered.transpose(1, 0, 2).reshape(rows, width)  1.58 us

profile of v4, /device:TPU:0, one launch (start us, length us, event | category | flops | bytes accessed | tf_op | source)
XLA Modules:
  0.0 39.1 jit_solution(207866356974709982)
XLA Ops:
  0.0 37.5 %shard_map.55 = bf16[4,24,768]{2,1,0:T(8,128)(2,1)} custom-call(bf16[24,3072]{1,0:T(8,128)(2,1)} %q_hbm.1, bf16[24,3072]{1,0:T(8,128)(2,1)} %k_hbm.1, bf16[24,3072]{1,0:T(8,128)(2,1)} %v_hbm.1, bf16[768,768]{1,0:T(8,128)(2,1)} %w_hbm.1, f32[4,1,768]{2,1,0:T(1,128)} %bitcast.5), custom_call_target="tpu_custom_call" | custom-call | tf_op jit(solution)/shard_map/pallas_call | solution.py:383
  37.5 1.6 %copy.7 = bf16[4,3,8,768]{3,2,0,1:T(8,128)(2,1)} copy(bf16[4,3,8,768]{3,2,1,0:T(8,128)(2,1)} %bitcast.4) | data formatting | bytes 294912 | tf_op jit(solution)/shard_map/reshape | solution.py:409
